TPU v7x, 32 devices: a whole 2x2x4 slice. The times are simulated.
32 devices in a mesh: fsdp: 4 (over z), ep: 8 (over y, x, core).
Axes of the slice: x: 2, y: 2, z: 4, core: 2. Of those that a mesh axis runs over, the one named last changes fastest.
Arguments:
- layer_in: bfloat16 [65536, 1024], P(('fsdp', 'ep'))
- out_grad: bfloat16 [65536, 1024], P(('fsdp', 'ep'))
- expert_ids: int32 [65536, 8], P(('fsdp', 'ep'))
- gate_vals: float32 [65536, 8], P(('fsdp', 'ep'))
- w_one: bfloat16 [32, 1024, 512], P('ep', 'fsdp')
- w_two: bfloat16 [32, 512, 1024], P('ep', None, 'fsdp')
- w_three: bfloat16 [32, 1024, 512], P('ep', 'fsdp')
Outputs:
- output 1: bfloat16 [65536, 1024], P(('fsdp', 'ep'))
- output 2: float32 [65536, 8], P(('fsdp', 'ep'))
- output 3: float32 [32, 1024, 512], P('ep', 'fsdp')
- output 4: float32 [32, 512, 1024], P('ep', None, 'fsdp')
- output 5: float32 [32, 1024, 512], P('ep', 'fsdp')
All inputs are finite; a program needn't handle non-finite values.
Results may differ from a plain program's by a relative error of at most 0.0103656.
Values are sent between devices in bfloat16 or wider.
A program may use at most 1 GiB of HBM per device.

v0:
```python
import jax
import jax.numpy as jnp
from jax import lax
from jax.sharding import PartitionSpec as P


def capacity_of(tok_dev, top_k, experts):
    return max(8, ((tok_dev * top_k * 5) // (4 * experts) + 7) // 8 * 8)


def route_slots(expert_ids, experts, capacity):
    flat_ids = expert_ids.reshape(-1)
    onehot = (flat_ids[:, None] == jnp.arange(experts, dtype=jnp.int32)[None, :]).astype(jnp.int32)
    before = jnp.cumsum(onehot, axis=0) - onehot
    position = jnp.sum(before * onehot, axis=1)
    return jnp.where(position < capacity, flat_ids * capacity + position, experts * capacity)


def slot_sources(slot_of, gate_vals, tok_dev, places):
    top_k = gate_vals.shape[-1]
    token_of = jnp.arange(slot_of.shape[0], dtype=jnp.int32) // top_k
    source = jnp.full((places,), tok_dev, jnp.int32).at[slot_of].set(token_of, mode="drop")
    slot_gate = jnp.zeros((places,), jnp.float32).at[slot_of].set(gate_vals.reshape(-1), mode="drop")
    return source, slot_gate


def take_rows(rows, row_index):
    return jnp.take(rows, row_index, axis=0, mode="fill", fill_value=0)


def expert_grads(x_rows, dy_rows, gate_rows, w_one, w_two, w_three):
    h_one = jnp.einsum("pecd,edf->pecf", x_rows, w_one, preferred_element_type=jnp.float32)
    h_three = jnp.einsum("pecd,edf->pecf", x_rows, w_three, preferred_element_type=jnp.float32)
    sig_one = jax.nn.sigmoid(h_one)
    silu_one = h_one * sig_one
    act_bf = (silu_one * h_three).astype(jnp.bfloat16)
    y_rows = jnp.einsum("pecf,efd->pecd", act_bf, w_two, preferred_element_type=jnp.float32)
    gate_grad = jnp.sum(dy_rows.astype(jnp.float32) * y_rows, axis=-1)
    g_rows = (gate_rows[..., None] * dy_rows.astype(jnp.float32)).astype(jnp.bfloat16)
    d_act = jnp.einsum("pecd,efd->pecf", g_rows, w_two, preferred_element_type=jnp.float32)
    dh_one = (d_act * h_three * sig_one * (1.0 + h_one * (1.0 - sig_one))).astype(jnp.bfloat16)
    dh_three = (d_act * silu_one).astype(jnp.bfloat16)
    dx_rows = (jnp.einsum("pecf,edf->pecd", dh_one, w_one, preferred_element_type=jnp.float32) + jnp.einsum("pecf,edf->pecd", dh_three, w_three, preferred_element_type=jnp.float32)).astype(jnp.bfloat16)
    grad_one = jnp.einsum("pecd,pecf->edf", x_rows, dh_one, preferred_element_type=jnp.float32)
    grad_three = jnp.einsum("pecd,pecf->edf", x_rows, dh_three, preferred_element_type=jnp.float32)
    grad_two = jnp.einsum("pecf,pecd->efd", act_bf, g_rows, preferred_element_type=jnp.float32)
    return dx_rows, gate_grad, grad_one, grad_two, grad_three


def solution(mesh):
    ep_size = mesh.shape["ep"]
    tok_spec = P(("fsdp", "ep"), None)
    up_spec = P("ep", "fsdp", None)
    down_spec = P("ep", None, "fsdp")

    def per_device(layer_in, out_grad, expert_ids, gate_vals, w_one, w_two, w_three):
        tok_dev, hidden = layer_in.shape
        top_k = expert_ids.shape[1]
        local_experts = w_one.shape[0]
        experts = local_experts * ep_size
        capacity = capacity_of(tok_dev, top_k, experts)
        places = experts * capacity
        slot_of = route_slots(expert_ids, experts, capacity)
        source, slot_gate = slot_sources(slot_of, gate_vals, tok_dev, places)
        send_shape = (ep_size, local_experts, capacity, hidden)
        x_send = take_rows(layer_in, source).reshape(send_shape)
        dy_send = take_rows(out_grad, source).reshape(send_shape)
        gate_send = slot_gate.reshape(ep_size, local_experts, capacity)
        x_rows = lax.all_to_all(x_send, "ep", 0, 0, tiled=True)
        dy_rows = lax.all_to_all(dy_send, "ep", 0, 0, tiled=True)
        gate_rows = lax.all_to_all(gate_send, "ep", 0, 0, tiled=True)
        w_one_full = lax.all_gather(w_one, "fsdp", axis=1, tiled=True)
        w_three_full = lax.all_gather(w_three, "fsdp", axis=1, tiled=True)
        w_two_full = lax.all_gather(w_two, "fsdp", axis=2, tiled=True)
        dx_rows, gate_grad, grad_one, grad_two, grad_three = expert_grads(x_rows, dy_rows, gate_rows, w_one_full, w_two_full, w_three_full)
        dx_back = lax.all_to_all(dx_rows, "ep", 0, 0, tiled=True).reshape(places, hidden)
        gate_back = lax.all_to_all(gate_grad, "ep", 0, 0, tiled=True).reshape(places)
        dx_pick = take_rows(dx_back, slot_of).reshape(tok_dev, top_k, hidden)
        in_grad = jnp.sum(dx_pick, axis=1, dtype=jnp.float32).astype(jnp.bfloat16)
        gate_out = take_rows(gate_back, slot_of).reshape(tok_dev, top_k)
        grad_one = lax.psum_scatter(grad_one, "fsdp", scatter_dimension=1, tiled=True)
        grad_three = lax.psum_scatter(grad_three, "fsdp", scatter_dimension=1, tiled=True)
        grad_two = lax.psum_scatter(grad_two, "fsdp", scatter_dimension=2, tiled=True)
        return in_grad, gate_out, grad_one, grad_two, grad_three

    return jax.shard_map(per_device, mesh=mesh, in_specs=(tok_spec, tok_spec, tok_spec, tok_spec, up_spec, down_spec, up_spec), out_specs=(tok_spec, tok_spec, up_spec, down_spec, up_spec), check_vma=False)
```

profile of v0, /device:TPU:0, one launch (start us, length us, event | category | flops | bytes accessed | tf_op | source)
XLA Modules:
  0.0 2416.6 jit_solution(12928095257678791694)
XLA Ops:
  7.2 1.2 copy.63
  8.4 0.5 eq.29
  8.9 0.5 eq.25
  9.4 0.1 broadcast_multiply_fusion
  9.4 0.1 copy.65
  9.5 0.5 mul.54
  10.1 1.2 copy.68
  11.2 0.5 reshape.146
  11.7 0.3 fusion.44
  12.0 0.3 reduce-window.9
  12.4 1.6 broadcast_add_fusion
  13.9 2.0 copy.66
  15.9 1.7 fusion.43
  17.7 0.6 copy-done.2
  18.3 0.1 compare_select_fusion.1
  18.4 60.4 %scatter_custom_fusion = f32[20480]{0:T(1024)S(1)} fusion(s32[16384]{0:T(1024)S(1)} %bitcast.112, f32[16384]{0:T(1024)S(1)} %reshape.146, f32[]{:T(128)} %constant.65.clone.1), kind=kCustom, calls=%fused_computation.79 | custom fusion | bytes 81924 | tf_op jit(solution)/shard_map/scatter | solution.py:23
  78.8 0.7 reshape.105
  79.5 5.2 all-to-all-start
  84.7 60.4 %scatter_custom_fusion.1 = s32[20480]{0:T(1024)S(1)} fusion(s32[16384]{0:T(1024)S(1)} %bitcast.113, s32[16384]{0:T(1024)S(1)} %add_select_fusion, s32[]{:T(128)} %constant.66.clone.1), kind=kCustom, calls=%fused_computation.77 | custom fusion | bytes 81924 | tf_op jit(solution)/shard_map/scatter | solution.py:22
  145.1 0.6 compare_and_fusion.1
  145.7 102.8 %gather_fusion.3 = bf16[20480,1024]{1,0:T(8,128)(2,1)} fusion(bf16[2048,1024]{1,0:T(8,128)(2,1)} %param.9, s32[20480]{0:T(1024)S(1)} %fusion.47), kind=kCustom, calls=%fused_computation.1.clone | custom fusion | bytes 83968000 | tf_op jit(solution)/shard_map/jit(_take)/gather | solution.py:28
  248.5 102.7 %gather_fusion.2 = bf16[20480,1024]{1,0:T(8,128)(2,1)} fusion(bf16[2048,1024]{1,0:T(8,128)(2,1)} %param.10, s32[20480]{0:T(1024)S(1)} %fusion.47), kind=kCustom, calls=%fused_computation.clone | custom fusion | bytes 83968000 | tf_op jit(solution)/shard_map/jit(_take)/gather | solution.py:28
  351.2 53.8 %broadcast_select_fusion.1 = (bf16[20480,1024]{1,0:T(8,128)(2,1)}, bf16[20480,1024]{1,0:T(8,128)(2,1)}) fusion(bf16[20480,1024]{1,0:T(8,128)(2,1)} %gather_fusion.2, pred[20480]{0:T(1024)(128)(4,1)S(1)} %copy-done.6, bf16[20480,1024]{1,0:T(8,128)(2,1)} %gather_fusion.3), kind=kLoop, calls=%fused_computation.28 | loop fusion | flops 41943040 | bytes 167792640 | tf_op jit(solution)/shard_map/jit(_take)/select_n | solution.py:28
  405.1 466.1 %all_to_all.25 = bf16[8,4,640,1024]{3,2,1,0:T(8,128)(2,1)} all-to-all(bf16[8,4,640,1024]{3,2,1,0:T(8,128)(2,1)} %bitcast.109), channel_id=1, replica_groups=mesh['fsdp'=4,'ep'=8] {'ep'}, dimensions={0} | all-to-all | bytes 83886080 | tf_op jit(solution)/shard_map/all_to_all | solution.py:69
  871.2 7.8 all-to-all-start.1
  879.0 0.0 all-gather.8.cloned.1.call-start
  879.1 0.7 all-gather.8.cloned.1.call-update
  879.7 0.0 all-gather.4.cloned.1.call-start
  879.8 0.7 all-gather.4.cloned.1.call-update
  880.5 0.0 all-gather.6.cloned.1.call-start
  880.5 0.7 all-gather.6.cloned.1.call-update
  881.2 0.3 reduce-scatter.6.cloned.1.call-start
  881.5 0.9 copy.69
  882.4 81.0 %all-gather.8.cloned.1.call-done = bf16[4,1024,512]{2,1,0:T(8,128)(2,1)} async-done(((bf16[4,256,512]{2,1,0:T(8,128)(2,1)}), bf16[4,1024,512]{2,1,0:T(8,128)(2,1)}) %all-gather.8.cloned.1.call-update) | async-done | bytes 4194320 | tf_op jit(solution)/shard_map/all_gather | solution.py:72
  963.4 36.9 %fusion.12 = f32[4,8,640,512]{3,2,1,0:T(8,128)} fusion(bf16[8,4,640,1024]{3,2,1,0:T(8,128)(2,1)} %all_to_all.25, bf16[4,1024,512]{2,1,0:T(8,128)(2,1)} %all-gather.8.cloned.1.call-done), kind=kOutput, calls=%fused_computation.29 | convolution fusion | flops 21474836480 | bytes 88080384 | tf_op jit(solution)/shard_map/pecd,edf->pecf/dot_general | solution.py:32
  1000.3 44.5 %all-gather.4.cloned.1.call-done = bf16[4,512,1024]{2,1,0:T(8,128)(2,1)} async-done(((bf16[4,512,256]{2,1,0:T(8,128)(2,1)}), bf16[4,512,1024]{2,1,0:T(8,128)(2,1)}) %all-gather.4.cloned.1.call-update) | async-done | bytes 4194320 | tf_op jit(solution)/shard_map/all_gather | solution.py:74
  1044.9 288.0 %all-to-all-done.1 = bf16[8,4,640,1024]{3,2,1,0:T(8,128)(2,1)} async-done(((bf16[8,4,640,1024]{3,2,1,0:T(8,128)(2,1)}), bf16[8,4,640,1024]{3,2,1,0:T(8,128)(2,1)}, u32[]{:S(2)}, u32[]{:S(2)}) %all-to-all-start.1) | async-done | bytes 41943072 | tf_op jit(solution)/shard_map/all_to_all | solution.py:70
  1332.9 37.8 %fusion.19 = f32[4,8,640,512]{3,2,1,0:T(8,128)} fusion(f32[8,4,640]{2,0,1:T(8,128)S(1)} %copy.69, bf16[8,4,640,1024]{3,2,1,0:T(8,128)(2,1)} %all-to-all-done.1, bf16[4,512,1024]{2,1,0:T(8,128)(2,1)} %all-gather.4.cloned.1.call-done), kind=kOutput, calls=%fused_computation.36 | convolution fusion | flops 21537751040 | bytes 88162304 | tf_op jit(solution)/shard_map/pecd,efd->pecf/dot_general | solution.py:40
  1370.7 68.6 %fusion.10 = (bf16[8,4,640,512]{3,2,0,1:T(8,128)(2,1)}, bf16[8,4,640,512]{3,2,0,1:T(8,128)(2,1)}, bf16[8,4,640,512]{3,2,0,1:T(8,128)(2,1)}) fusion(f32[4,8,640,512]{3,2,1,0:T(8,128)} %fusion.12, f32[4,8,640,512]{3,2,1,0:T(8,128)} %fusion.19, bf16[4,1024,512]{2,1,0:T(8,128)(2,1)} %all-gather.6.cloned.1.call-done, bf16[8,4,640,1024]{3,2,1,0:T(8,128)(2,1)} %all_to_all.25), kind=kOutput, calls=%fused_computation.24 | convolution fusion | flops 21632122880 | bytes 192937984 | tf_op jit(solution)/shard_map/pecd,edf->pecf/dot_general | solution.py:33
  1439.3 29.7 %fusion.1 = f32[8,4,640]{2,0,1:T(8,128)S(1)} fusion(bf16[8,4,640,1024]{3,2,1,0:T(8,128)(2,1)} %all-to-all-done.1, bf16[8,4,640,512]{3,2,0,1:T(8,128)(2,1)} %get-tuple-element.28, bf16[4,512,1024]{2,1,0:T(8,128)(2,1)} %all-gather.4.cloned.1.call-done), kind=kOutput, calls=%fused_computation.9 | convolution fusion | flops 21537730560 | bytes 67190784 | tf_op jit(solution)/shard_map/pecf,efd->pecd/dot_general | solution.py:37
  1469.0 0.7 copy.74
  1469.7 30.8 %fusion.38 = f32[4,512,1024]{2,1,0:T(8,128)} fusion(bf16[8,4,640,512]{3,2,0,1:T(8,128)(2,1)} %get-tuple-element.28, f32[8,4,640]{2,0,1:T(8,128)S(1)} %copy-done.8, bf16[8,4,640,1024]{3,2,1,0:T(8,128)(2,1)} %all-to-all-done.1), kind=kOutput, calls=%fused_computation.50 | convolution fusion | flops 21537751040 | bytes 71385088 | tf_op jit(solution)/shard_map/pecf,pecd->efd/dot_general | solution.py:46
  1500.5 0.0 reduce-scatter.6.cloned.1.call-update
  1500.5 3.6 all-to-all-start.4
  1504.1 40.4 %fusion.25 = f32[4,8,640,1024]{3,2,1,0:T(8,128)} fusion(bf16[8,4,640,512]{3,2,0,1:T(8,128)(2,1)} %get-tuple-element.29, bf16[4,1024,512]{2,1,0:T(8,128)(2,1)} %all-gather.8.cloned.1.call-done), kind=kOutput, calls=%fused_computation.41 | convolution fusion | flops 21474836480 | bytes 109051904 | tf_op jit(solution)/shard_map/pecf,edf->pecd/dot_general | solution.py:43
  1544.5 49.7 %fusion.2 = bf16[8,4,640,1024]{3,2,0,1:T(8,128)(2,1)} fusion(f32[4,8,640,1024]{3,2,1,0:T(8,128)} %fusion.25, bf16[8,4,640,512]{3,2,0,1:T(8,128)(2,1)} %get-tuple-element.30, bf16[4,1024,512]{2,1,0:T(8,128)(2,1)} %all-gather.6.cloned.1.call-done), kind=kOutput, calls=%fused_computation.11 | convolution fusion | flops 21516779520 | bytes 150994944 | tf_op jit(solution)/shard_map/pecf,edf->pecd/dot_general | solution.py:43
  1594.2 28.4 %copy.73 = bf16[8,4,640,1024]{3,2,1,0:T(8,128)(2,1)} copy(bf16[8,4,640,1024]{3,2,0,1:T(8,128)(2,1)} %fusion.2) | data formatting | bytes 83886080 | tf_op jit(solution)/shard_map/convert_element_type | solution.py:43
  1622.6 7.8 all-to-all-start.3
  1630.4 0.0 reduce-scatter.8.cloned.1.call-start
  1630.5 31.4 %fusion.35 = f32[4,1024,512]{2,1,0:T(8,128)} fusion(bf16[8,4,640,1024]{3,2,1,0:T(8,128)(2,1)} %all_to_all.25, bf16[8,4,640,512]{3,2,0,1:T(8,128)(2,1)} %get-tuple-element.30), kind=kOutput, calls=%fused_computation.49 | convolution fusion | flops 21474836480 | bytes 71303168 | tf_op jit(solution)/shard_map/pecd,pecf->edf/dot_general | solution.py:45
  1661.9 0.0 reduce-scatter.8.cloned.1.call-update
  1661.9 0.0 copy-start.5
  1661.9 0.0 reduce-scatter.4.cloned.1.call-start
  1662.0 30.9 %fusion.32 = f32[4,1024,512]{2,1,0:T(8,128)} fusion(bf16[8,4,640,1024]{3,2,1,0:T(8,128)(2,1)} %all_to_all.25, bf16[8,4,640,512]{3,2,0,1:T(8,128)(2,1)} %get-tuple-element.29), kind=kOutput, calls=%fused_computation.48 | convolution fusion | flops 21474836480 | bytes 71303168 | tf_op jit(solution)/shard_map/pecd,pecf->edf/dot_general | solution.py:44
  1692.9 0.0 reduce-scatter.4.cloned.1.call-update
  1692.9 0.6 reduce_sum.35
  1693.6 0.0 copy-start.1
  1693.6 90.5 %gather_fusion.1 = f32[16384]{0:T(1024)S(1)} fusion(f32[20480]{0:T(1024)S(1)} %reshape.109, s32[16384]{0:T(1024)S(1)} %broadcast_clamp_fusion), kind=kCustom, calls=%fused_computation.3 | custom fusion | bytes 196608 | tf_op jit(solution)/shard_map/jit(_take)/gather | solution.py:28
  1784.1 0.6 gather.18
  1784.7 1.4 broadcast_select_fusion.2
  1786.1 2.2 copy.80
  1788.3 296.0 %all-to-all-done.3 = bf16[8,4,640,1024]{3,2,1,0:T(8,128)(2,1)} async-done(((bf16[8,4,640,1024]{3,2,1,0:T(8,128)(2,1)}), bf16[8,4,640,1024]{3,2,1,0:T(8,128)(2,1)}, u32[]{:S(2)}, u32[]{:S(2)}) %all-to-all-start.3) | async-done | bytes 41943072 | tf_op jit(solution)/shard_map/all_to_all | solution.py:76
  2084.3 300.9 %gather_fusion = bf16[16384,1024]{1,0:T(8,128)(2,1)} fusion(bf16[20480,1024]{1,0:T(8,128)(2,1)} %bitcast.17, s32[16384]{0:T(1024)S(1)} %broadcast_clamp_fusion), kind=kCustom, calls=%fused_computation.2 | custom fusion | bytes 67174400 | tf_op jit(solution)/shard_map/jit(_take)/gather | solution.py:28
  2385.2 24.1 fusion.16
  (27 shorter events, 0.2 us)
Async XLA Ops:
  8.3 240.2 %copy-start = (s32[2048,8]{1,0:T(8,128)}, s32[2048,8]{1,0:T(8,128)S(1)}, u32[]{:S(2)}) copy-start(s32[2048,8]{1,0:T(8,128)S(1)} %copy.63) | copy-start | bytes 196612
  17.7 0.6 copy-start.2
  18.4 230.1 %copy-start.4 = (s32[16384,1]{0,1:T(1,128)}, s32[16384,1]{0,1:T(1,128)S(1)}, u32[]{:S(2)}) copy-start(s32[16384,1]{0,1:T(1,128)S(1)} %compare_select_fusion.1) | copy-start | bytes 196612
  79.5 325.6 %all-to-all-start = ((f32[8,4,640]{2,1,0:T(4,128)}), f32[8,4,640]{2,1,0:T(4,128)}, u32[]{:S(2)}, u32[]{:S(2)}) async-start(f32[8,4,640]{2,1,0:T(4,128)} %reshape.105), calls=%async_computation | async-start | bytes 163840 | tf_op jit(solution)/shard_map/all_to_all | solution.py:71
  248.5 102.7 %copy-start.6 = (pred[20480]{0:T(1024)(128)(4,1)S(1)}, pred[20480]{0:T(1024)(128)(4,1)}, u32[]{:S(2)}) copy-start(pred[20480]{0:T(1024)(128)(4,1)} %compare_and_fusion.1) | copy-start | bytes 61444
  871.2 461.7 %all-to-all-start.1 = ((bf16[8,4,640,1024]{3,2,1,0:T(8,128)(2,1)}), bf16[8,4,640,1024]{3,2,1,0:T(8,128)(2,1)}, u32[]{:S(2)}, u32[]{:S(2)}) async-start(bf16[8,4,640,1024]{3,2,1,0:T(8,128)(2,1)} %bitcast.108), calls=%async_computation.1 | async-start | bytes 83886080 | tf_op jit(solution)/shard_map/all_to_all | solution.py:70
  879.0 84.4 %all-gather.8.cloned.1.call-start = ((), (), s32[]{:S(2)}) async-start(), calls=%async_computation.10 | async-start | bytes 5242880 | tf_op jit(solution)/shard_map/all_gather | solution.py:72
  879.7 165.1 %all-gather.4.cloned.1.call-start = ((), (), s32[]{:S(2)}) async-start(), calls=%async_computation.8 | async-start | bytes 5242880 | tf_op jit(solution)/shard_map/all_gather | solution.py:74
  880.5 490.2 %all-gather.6.cloned.1.call-start = ((), (), s32[]{:S(2)}) async-start(), calls=%async_computation.9 | async-start | bytes 5242880 | tf_op jit(solution)/shard_map/all_gather | solution.py:73
  881.2 1528.1 %reduce-scatter.6.cloned.1.call-start = ((), (), s32[]{:S(2)}) async-start(), calls=%async_computation.12 | async-start | bytes 10485760 | tf_op jit(solution)/shard_map/reduce_scatter | solution.py:83
  882.4 450.5 %copy-start.7 = (f32[8,4,640]{2,0,1:T(8,128)}, f32[8,4,640]{2,0,1:T(8,128)S(1)}, u32[]{:S(2)}) copy-start(f32[8,4,640]{2,0,1:T(8,128)S(1)} %copy.69) | copy-start | bytes 245764
  1439.3 30.4 %copy-start.8 = (f32[8,4,640]{2,0,1:T(8,128)S(1)}, f32[8,4,640]{2,0,1:T(8,128)}, u32[]{:S(2)}) copy-start(f32[8,4,640]{2,0,1:T(8,128)} %copy-done.7) | copy-start | bytes 245764
  1500.5 122.1 %all-to-all-start.4 = ((f32[8,4,640]{2,1,0:T(4,128)}), f32[8,4,640]{2,1,0:T(4,128)S(1)}, u32[]{:S(2)}, u32[]{:S(2)}) async-start(f32[8,4,640]{2,1,0:T(4,128)} %copy.74), calls=%async_computation.4 | async-start | bytes 163840 | tf_op jit(solution)/shard_map/all_to_all | solution.py:77
  1622.6 461.7 %all-to-all-start.3 = ((bf16[8,4,640,1024]{3,2,1,0:T(8,128)(2,1)}), bf16[8,4,640,1024]{3,2,1,0:T(8,128)(2,1)}, u32[]{:S(2)}, u32[]{:S(2)}) async-start(bf16[8,4,640,1024]{3,2,1,0:T(8,128)(2,1)} %copy.73), calls=%async_computation.3 | async-start | bytes 83886080 | tf_op jit(solution)/shard_map/all_to_all | solution.py:76
  1630.4 778.9 %reduce-scatter.8.cloned.1.call-start = ((), (), s32[]{:S(2)}) async-start(), calls=%async_computation.13 | async-start | bytes 10485760 | tf_op jit(solution)/shard_map/reduce_scatter | solution.py:82
  1661.9 31.0 %copy-start.3 = (s32[16384]{0:T(1024)S(1)}, s32[16384]{0:T(1024)}, u32[]{:S(2)}) copy-start(s32[16384]{0:T(1024)} %copy-done.2) | copy-start | bytes 196612
  1661.9 31.6 %copy-start.5 = (s32[16384,1]{0,1:T(1,128)S(1)}, s32[16384,1]{0,1:T(1,128)}, u32[]{:S(2)}) copy-start(s32[16384,1]{0,1:T(1,128)} %copy-done.4) | copy-start | bytes 196612
  1661.9 747.4 %reduce-scatter.4.cloned.1.call-start = ((), (), s32[]{:S(2)}) async-start(), calls=%async_computation.11 | async-start | bytes 10485760 | tf_op jit(solution)/shard_map/reduce_scatter | solution.py:81
  1693.6 91.1 %copy-start.1 = (s32[2048,8]{1,0:T(8,128)S(1)}, s32[2048,8]{1,0:T(8,128)}, u32[]{:S(2)}) copy-start(s32[2048,8]{1,0:T(8,128)} %copy-done) | copy-start | bytes 196612
Sparse Core Ops, SparseCore 0:
  881.4 81.9 all-gather.7
  965.0 79.8 all-gather.3
  1046.4 77.7 all-gather.5
  1500.6 143.9 reduce-scatter.5
  1662.0 146.0 reduce-scatter.7
  1810.9 144.6 reduce-scatter.3
where the time goes:
time: 2430 us; the launch traced here: 2420 us
  local copies, waits for them, and re-layouts  759 us (31%)
  waiting for transfers between devices  712 us (29%)
  blocking collectives  466 us (19%)
  matrix products  356 us (15%)
  other arithmetic  84.1 us (3%)
  starting transfers between devices  24.9 us (1%)
    gather x5, local copies, waits for them, and re-layouts, take_rows(): return jnp.take(rows, row_index, axis=0, mode='fill', fill_value=0)  597 us
    all_to_all x1, blocking collectives, per_device(): x_rows = lax.all_to_all(x_send, 'ep', 0, 0, tiled=True)  466 us
    all_to_all x1, waiting for transfers between devices, per_device(): lax.all_to_all(dx_rows, 'ep', 0, 0, tiled=True).reshape(places, hidden)  296 us
    all_to_all x1, waiting for transfers between devices, per_device(): dy_rows = lax.all_to_all(dy_send, 'ep', 0, 0, tiled=True)  288 us
    all_gather x1, waiting for transfers between devices, per_device(): w_one_full = lax.all_gather(w_one, 'fsdp', axis=1, tiled=True)  81 us
    dot_general x1, matrix products, expert_grads(): jnp.einsum('pecd,edf->pecf', x_rows, w_three, preferred_element_type=jnp....  68.6 us
    scatter x1, local copies, waits for them, and re-layouts, slot_sources(): jnp.zeros((places,), jnp.float32).at[slot_of]  60.4 us
    scatter x1, local copies, waits for them, and re-layouts, slot_sources(): jnp.full((places,), tok_dev, jnp.int32).at[slot_of]  60.4 us
  transfers between devices with their start and end apart: 10, of which 4 were waited for; matrix products, arithmetic and copies ran while one was open for 41% of the time, Pallas kernels for 0%

commit v1 on v0

v1 whole, which is shorter than its diff:
```python
import functools

import jax
import jax.numpy as jnp
from jax import lax
from jax.experimental import pallas as pl
from jax.experimental.pallas import tpu as pltpu
from jax.sharding import PartitionSpec as P

TILE = 256
ALIGN = 16
WIN = TILE + ALIGN
BACK = TILE - ALIGN
F32 = jnp.float32
BF16 = jnp.bfloat16


def capacity_of(tok_dev, top_k, experts):
    return max(8, ((tok_dev * top_k * 5) // (4 * experts) + 7) // 8 * 8)


def dot_nn(a, b):
    return lax.dot_general(a, b, (((1,), (0,)), ((), ())), preferred_element_type=F32)


def dot_nt(a, b):
    return lax.dot_general(a, b, (((1,), (1,)), ((), ())), preferred_element_type=F32)


def dot_tn(a, b):
    return lax.dot_general(a, b, (((0,), (0,)), ((), ())), preferred_element_type=F32)


def expert_kernel(first, capacity, rows_blk, starts, pos, gate, xa, xb, ya, yb, w_up, w_down, *rest):
    if first:
        dx, dgate, g_up, g_down = rest[:4]
        scratch = rest[4:]
    else:
        acc_up, acc_down, dx, dgate, g_up, g_down = rest[:6]
        scratch = rest[6:]
    xbuf, ybuf, xs, us, gs, dgs, dhs, acts, sems = scratch
    step = pl.program_id(0)
    tok = xbuf.shape[1]
    hidden = xbuf.shape[2]
    ff = acts.shape[1]
    tiles = tok // TILE

    def copies(src):
        x_ref, y_ref = ((xa, ya), (xb, yb))[src]
        return (pltpu.make_async_copy(x_ref, xbuf.at[src], sems.at[src, 0]),
                pltpu.make_async_copy(y_ref, ybuf.at[src], sems.at[src, 1]))

    @pl.when(step == 0)
    def _():
        for src in range(2):
            for cp in copies(src):
                cp.start()

    if first:
        g_up[...] = jnp.zeros_like(g_up)
        g_down[...] = jnp.zeros_like(g_down)
    else:
        g_up[...] = acc_up[...]
        g_down[...] = acc_down[...]

    @pl.when(step == 0)
    def _():
        for src in range(2):
            for cp in copies(src):
                cp.wait()

    slot_iota = lax.broadcasted_iota(jnp.int32, (WIN, TILE), 0)

    def source_body(src, carry):
        xs[0:capacity, :] = jnp.zeros((capacity, hidden), BF16)
        us[0:capacity, :] = jnp.zeros((capacity, hidden), BF16)
        gs[0:capacity, :] = jnp.zeros((capacity, 128), F32)

        def pick(i, carry):
            start = pl.multiple_of(starts[step, src, i], ALIGN)
            pos_row = pos[0, src, pl.ds(i, 1), :]
            gate_row = gate[0, src, pl.ds(i, 1), :]
            hit = (slot_iota + start) == pos_row
            onehot = jnp.where(hit, 1.0, 0.0).astype(BF16)
            tok0 = pl.multiple_of(i * TILE, TILE)
            for buf, rows in ((xbuf, xs), (ybuf, us)):
                for c in range(0, hidden, 256):
                    got = dot_nn(onehot, buf[src, pl.ds(tok0, TILE), c:c + 256]).astype(BF16)
                    rows[pl.ds(start, ALIGN), c:c + 256] = rows[pl.ds(start, ALIGN), c:c + 256] + got[:ALIGN]
                    rows[pl.ds(start + ALIGN, TILE), c:c + 256] = got[ALIGN:]
            got_gate = jnp.sum(jnp.where(hit, gate_row, 0.0), axis=1, keepdims=True)
            got_gate = jnp.broadcast_to(got_gate, (WIN, 128))
            gs[pl.ds(start, ALIGN), :] = gs[pl.ds(start, ALIGN), :] + got_gate[:ALIGN]
            gs[pl.ds(start + ALIGN, TILE), :] = got_gate[ALIGN:]
            return carry

        lax.fori_loop(0, tiles, pick, 0)

        def rows_body(b, carry):
            r0 = pl.multiple_of(b * rows_blk, rows_blk)
            rows = pl.ds(r0, rows_blk)
            up = w_up[...].reshape(hidden, 2 * ff)
            down = w_down[...].reshape(hidden, ff)
            h = dot_nn(xs[rows, :], up)
            h_one = h[:, :ff]
            h_three = h[:, ff:]
            sig = jax.nn.sigmoid(h_one)
            silu = h_one * sig
            act = (silu * h_three).astype(BF16)
            acts[rows, :] = act
            u = us[rows, :].astype(F32)
            y = dot_nt(act, down)
            dg = jnp.sum(u * y, axis=1, keepdims=True)
            dgs[rows, :] = jnp.broadcast_to(dg, (rows_blk, 128))
            g = (gs[rows, 0:1] * u).astype(BF16)
            us[rows, :] = g
            da = dot_nn(g, down)
            dh_one = (da * h_three * sig * (1.0 + h_one * (1.0 - sig))).astype(BF16)
            dh_three = (da * silu).astype(BF16)
            dhs[rows, 0:ff] = dh_one
            dhs[rows, ff:2 * ff] = dh_three
            dx[0, src, rows, :] = dot_nt(dhs[rows, :], up).astype(BF16)
            return carry

        lax.fori_loop(0, capacity // rows_blk, rows_body, 0)

        quarter = g_up.shape[2]
        for z in range(g_up.shape[0]):
            cols = slice(z * quarter, (z + 1) * quarter)
            g_up[z, 0] += dot_tn(xs[0:capacity, cols], dhs[...])
            g_down[z, 0] += dot_tn(us[0:capacity, cols], acts[...])

        def give(i, carry):
            start = pl.multiple_of(starts[step, src, i], ALIGN)
            hit = (slot_iota + start) == pos[0, src, pl.ds(i, 1), :]
            val = dgs[pl.ds(start, WIN), :]
            val = jnp.concatenate([val, val], axis=1)
            dgate[0, src, pl.ds(i, 1), :] = jnp.sum(jnp.where(hit, val, 0.0), axis=0, keepdims=True)
            return carry

        lax.fori_loop(0, tiles, give, 0)
        return carry

    lax.fori_loop(0, 2, source_body, 0)


def run_experts(starts, pos, gate, xa, xb, ya, yb, w_up, w_down, acc):
    n_exp, _, tiles, _ = pos.shape
    tok, hidden = xa.shape
    parts, _, quarter, two_ff = w_up.shape
    ff = two_ff // 2
    capacity = run_experts.capacity
    first = acc is None
    rows_blk = capacity // 2 if capacity % 32 == 0 else capacity
    padded = capacity + WIN
    any_spec = pl.BlockSpec(memory_space=pl.ANY)
    tok_spec = pl.BlockSpec((1, 2, tiles, TILE), lambda e, s: (e, 0, 0, 0))
    once = pl.Buffered(1)
    up_spec = pl.BlockSpec((parts, 1, quarter, two_ff), lambda e, s: (0, e, 0, 0))
    down_spec = pl.BlockSpec((parts, 1, quarter, ff), lambda e, s: (0, e, 0, 0))
    up_once = pl.BlockSpec((parts, 1, quarter, two_ff), lambda e, s: (0, e, 0, 0), pipeline_mode=once)
    down_once = pl.BlockSpec((parts, 1, quarter, ff), lambda e, s: (0, e, 0, 0), pipeline_mode=once)
    in_specs = [tok_spec, tok_spec] + [any_spec] * 4 + [up_spec, down_spec]
    args = [starts, pos, gate, xa, xb, ya, yb, w_up, w_down]
    if not first:
        in_specs += [up_once, down_once]
        args += list(acc)
    flops = n_exp * 2 * (9 * capacity * hidden * ff + 2 * WIN * tok * hidden) * 2
    return pl.pallas_call(
        functools.partial(expert_kernel, first, capacity, rows_blk),
        grid_spec=pltpu.PrefetchScalarGridSpec(
            num_scalar_prefetch=1,
            grid=(n_exp,),
            in_specs=in_specs,
            out_specs=[pl.BlockSpec((1, 2, capacity, hidden), lambda e, s: (e, 0, 0, 0)), tok_spec, up_spec, down_spec],
            scratch_shapes=[
                pltpu.VMEM((2, tok, hidden), BF16),
                pltpu.VMEM((2, tok, hidden), BF16),
                pltpu.VMEM((padded, hidden), BF16),
                pltpu.VMEM((padded, hidden), BF16),
                pltpu.VMEM((padded, 128), F32),
                pltpu.VMEM((padded, 128), F32),
                pltpu.VMEM((capacity, two_ff), BF16),
                pltpu.VMEM((capacity, ff), BF16),
                pltpu.SemaphoreType.DMA((2, 2)),
            ],
        ),
        out_shape=[
            jax.ShapeDtypeStruct((n_exp, 2, capacity, hidden), BF16),
            jax.ShapeDtypeStruct((n_exp, 2, tiles, TILE), F32),
            jax.ShapeDtypeStruct((parts, n_exp, quarter, two_ff), F32),
            jax.ShapeDtypeStruct((parts, n_exp, quarter, ff), F32),
        ],
        compiler_params=pltpu.CompilerParams(dimension_semantics=("arbitrary",), vmem_limit_bytes=66 * 1024 * 1024 - 2 ** 21),
        cost_estimate=pl.CostEstimate(flops=flops, bytes_accessed=90 * 2 ** 20, transcendentals=0),
        name="experts",
    )(*args)


def combine_kernel(n_arr, back_tok, capacity, starts, pos, *rest):
    dxs = rest[:n_arr]
    out = rest[n_arr]
    src = pl.program_id(0)
    lane = lax.broadcasted_iota(jnp.int32, (BACK, TILE), 1)
    per = dxs[0].shape[0]

    def body(i, carry):
        tok0 = pl.multiple_of(jnp.minimum(i * BACK, back_tok), ALIGN)
        total = None
        for e in range(n_arr * per):
            start = pl.multiple_of(starts[src, e, i], ALIGN)
            hit = (lane + start) == pos[0, pl.ds(tok0, BACK), e:e + 1]
            onehot = jnp.where(hit, 1.0, 0.0).astype(BF16)
            term = dot_nn(onehot, dxs[e // per][e % per, 0, pl.ds(start, TILE), :])
            total = term if total is None else total + term
        out[0, pl.ds(tok0, BACK), :] = total.astype(BF16)
        return carry

    lax.fori_loop(0, starts.shape[2], body, 0)


def run_combine(starts, pos, dxs):
    per, _, capacity, hidden = dxs[0].shape
    tok = pos.shape[1]
    n_exp = per * len(dxs)
    return pl.pallas_call(
        functools.partial(combine_kernel, len(dxs), tok - BACK, capacity),
        grid_spec=pltpu.PrefetchScalarGridSpec(
            num_scalar_prefetch=1,
            grid=(2,),
            in_specs=[pl.BlockSpec((1, tok, n_exp), lambda s, st: (s, 0, 0))]
            + [pl.BlockSpec((per, 1, capacity, hidden), lambda s, st: (0, s, 0, 0)) for _ in dxs],
            out_specs=pl.BlockSpec((1, tok, hidden), lambda s, st: (s, 0, 0)),
        ),
        out_shape=jax.ShapeDtypeStruct((2, tok, hidden), BF16),
        compiler_params=pltpu.CompilerParams(dimension_semantics=("arbitrary",), vmem_limit_bytes=48 * 2 ** 20),
        cost_estimate=pl.CostEstimate(flops=2 * n_exp * tok * TILE * hidden * 2, bytes_accessed=20 * 2 ** 20, transcendentals=0),
        name="combine",
    )(starts, pos, *dxs)


def places_of(ids, gates, base, local_experts, capacity):
    n, _, tok = ids.shape
    tiles = tok // TILE
    want = base + jnp.arange(local_experts, dtype=jnp.int32)
    same = ids[:, None, :, :] == want[None, :, None, None]
    gate = jnp.sum(jnp.where(same, gates[:, None, :, :], 0.0), axis=2)
    hit = jnp.any(same, axis=2)
    rows = hit.reshape(n * local_experts * tiles, TILE).astype(BF16)
    upper = (jnp.arange(TILE)[:, None] < jnp.arange(TILE)[None, :]).astype(BF16)
    inside = jnp.dot(rows, upper, preferred_element_type=F32)
    count = jnp.sum(rows.astype(F32), axis=1).reshape(n, local_experts, tiles)
    before = (jnp.arange(tiles)[:, None] < jnp.arange(tiles)[None, :]).astype(F32)
    first = jnp.sum(count[..., :, None] * before, axis=2)
    place = (inside.reshape(n, local_experts, tiles, TILE) + first[..., None]).astype(jnp.int32)
    kept = hit.reshape(n, local_experts, tiles, TILE) & (place < capacity)
    return place, jnp.where(kept, place, -1), gate.reshape(n, local_experts, tiles, TILE)


def solution(mesh):
    ep_size = mesh.shape["ep"]
    tok_spec = P(("fsdp", "ep"), None)
    up_spec = P("ep", "fsdp", None)
    down_spec = P("ep", None, "fsdp")

    def swap(a, mask):
        return lax.ppermute(a, "ep", [(i, i ^ mask) for i in range(ep_size)])

    def add2(a, b):
        return (a.astype(F32) + b.astype(F32)).astype(BF16)

    def per_device(layer_in, out_grad, expert_ids, gate_vals, w_one, w_two, w_three):
        tok, hidden = layer_in.shape
        top_k = expert_ids.shape[1]
        local_experts = w_one.shape[0]
        experts = local_experts * ep_size
        capacity = capacity_of(tok, top_k, experts)
        run_experts.capacity = capacity
        me = lax.axis_index("ep")
        half = local_experts // 2

        x_of = {0: layer_in}
        y_of = {0: out_grad}
        x_of[1], y_of[1] = swap(layer_in, 1), swap(out_grad, 1)
        x_of[2], y_of[2] = swap(layer_in, 2), swap(out_grad, 2)
        x_of[4], y_of[4] = swap(layer_in, 4), swap(out_grad, 4)
        x_of[6], y_of[6] = swap(x_of[2], 4), swap(y_of[4], 2)
        for m in (2, 4, 6):
            x_of[m + 1], y_of[m + 1] = swap(x_of[m], 1), swap(y_of[m], 1)

        up_loc = jnp.concatenate([w_one, w_three], axis=2)
        down_loc = jnp.swapaxes(w_two, 1, 2)
        w_up, w_down = [], []
        for h in range(2):
            w_up.append(lax.all_gather(up_loc[h * half:(h + 1) * half], "fsdp", axis=0))
            w_down.append(lax.all_gather(down_loc[h * half:(h + 1) * half], "fsdp", axis=0))

        ids_t = expert_ids.T
        table = jnp.concatenate([ids_t.astype(F32), gate_vals.T], axis=0)
        tables = lax.all_gather(table, "ep", axis=0)
        tables = jnp.take(tables, me ^ jnp.arange(ep_size, dtype=jnp.int32), axis=0)
        ids = tables[:, :top_k].astype(jnp.int32)
        place, kept, gate = places_of(ids, tables[:, top_k:], me * local_experts, local_experts, capacity)
        first_place = jnp.minimum(place[..., 0], capacity) // ALIGN * ALIGN
        flat_place = place.reshape(ep_size, local_experts, tok)
        n_back = -(-tok // BACK)
        back_at = [min(i * BACK, tok - BACK) for i in range(n_back)]
        back_place = jnp.stack([flat_place[..., t] for t in back_at], axis=-1)
        back_place = jnp.minimum(back_place // ALIGN * ALIGN, capacity - TILE)
        kept_cols = jnp.swapaxes(kept.reshape(ep_size, local_experts, tok), 1, 2)

        def call(k, h, acc):
            m = 2 * k
            es = slice(h * half, (h + 1) * half)
            put = lambda a: jnp.swapaxes(a[m:m + 2, es], 0, 1)
            return run_experts(put(first_place), put(kept), put(gate), x_of[m], x_of[m + 1], y_of[m], y_of[m + 1], w_up[h], w_down[h], acc)

        acc = [None, None]
        dx_of = {}
        dg_of = {}
        sent = {}

        def expert_part(k, h):
            dx, dg, a_up, a_down = call(k, h, acc[h])
            acc[h] = (a_up, a_down)
            dx_of[k, h] = dx
            dg_of[k, h] = dg

        def back_part(k):
            m = 2 * k
            part = run_combine(back_place[m:m + 2], kept_cols[m:m + 2], [dx_of[k, 0], dx_of[k, 1]])
            other = swap(part[1], 1)
            if k == 0:
                sent[0] = (part[0], other)
            else:
                sent[k] = (swap(add2(part[0], other), m),)

        expert_part(0, 0)
        expert_part(0, 1)
        back_part(0)
        expert_part(1, 0)
        expert_part(1, 1)
        back_part(1)
        expert_part(2, 0)
        expert_part(3, 0)
        g_up = [None, None]
        g_down = [None, None]

        def reduce_part(h):
            g_up[h] = lax.psum_scatter(acc[h][0], "fsdp", scatter_dimension=0, tiled=False)
            g_down[h] = lax.psum_scatter(acc[h][1], "fsdp", scatter_dimension=0, tiled=False)

        reduce_part(0)
        expert_part(2, 1)
        back_part(2)
        expert_part(3, 1)
        back_part(3)
        reduce_part(1)

        terms = [t for k in range(ep_size // 2) for t in sent[k]]
        in_grad = functools.reduce(lambda a, b: a + b, [t.astype(F32) for t in terms]).astype(BF16)

        dg = jnp.concatenate([jnp.concatenate([dg_of[k, h] for h in range(2)], axis=0) for k in range(ep_size // 2)], axis=1)
        dg = jnp.swapaxes(dg, 0, 1).reshape(ep_size, local_experts, tok)
        dg = jnp.take(dg, me ^ jnp.arange(ep_size, dtype=jnp.int32), axis=0)
        dg = lax.all_to_all(dg, "ep", 0, 0, tiled=True).reshape(experts, tok)
        pick = ids_t[:, None, :] == jnp.arange(experts, dtype=jnp.int32)[None, :, None]
        gate_out = jnp.sum(jnp.where(pick, dg[None], 0.0), axis=1).T

        up = jnp.concatenate(g_up, axis=0)
        down = jnp.swapaxes(jnp.concatenate(g_down, axis=0), 1, 2)
        ff = w_one.shape[2]
        return in_grad, gate_out, up[:, :, :ff], down, up[:, :, ff:]

    return jax.shard_map(per_device, mesh=mesh, in_specs=(tok_spec, tok_spec, tok_spec, tok_spec, up_spec, down_spec, up_spec), out_specs=(tok_spec, tok_spec, up_spec, down_spec, up_spec), check_vma=False)
```

time: 2430 us -> 1170 us (0.48)
  local copies, waits for them, and re-layouts: 759 us -> 43.8 us
  Pallas kernels: 0 us -> 621 us
  waiting for transfers between devices: 712 us -> 248 us
  matrix products: 356 us -> 0.24 us
  blocking collectives: 466 us -> 177 us
  other arithmetic: 84.1 us -> 42 us
    pallas_call x0 -> x12, Pallas kernels: none -> 621 us  [the longest x8 548 us: run_experts(): pl.pallas_call(functools.partial(expert_kernel, first, capacity, rows_blk...]
    gather x5 -> x2, local copies, waits for them, and re-layouts: 597 us -> 2.66 us  [the longest x1 1.84 us: per_device(): tables = jnp.take(tables, me ^ jnp.arange(ep_size, dtype=jnp.int32), axis=0)]
    all_to_all x4 -> x0, waiting for transfers between devices: 584 us -> none  [the longest x1 296 us: per_device(): lax.all_to_all(dx_rows, 'ep', 0, 0, tiled=True).reshape(places, hidden)]
    dot_general x9 -> x1, matrix products: 356 us -> 0.24 us  [places_of(): inside = jnp.dot(rows, upper, preferred_element_type=F32)]
    all_to_all x1, blocking collectives: 466 us -> 177 us  [per_device(): dg = lax.all_to_all(dg, 'ep', 0, 0, tiled=True).reshape(experts, tok)]
    ppermute x0 -> x21, waiting for transfers between devices: none -> 147 us  [swap(): return lax.ppermute(a, 'ep', [(i, i ^ mask) for i in range(ep_size)])]
    scatter x2 -> x0, local copies, waits for them, and re-layouts: 121 us -> none  [the longest x1 60.4 us: slot_sources(): jnp.zeros((places,), jnp.float32).at[slot_of]]
    all_gather x3 -> x5, waiting for transfers between devices: 126 us -> 48.7 us  [the longest x2 28.3 us: per_device(): w_up.append(lax.all_gather(up_loc[h * half:(h + 1) * half], 'fsdp', axis=0))]
  transfers between devices with their start and end apart: 10 -> 30, of which waited for: 4 -> 5; matrix products, arithmetic and copies ran while one was open for 41% -> 7% of each run, Pallas kernels for 0% -> 47%
where the time goes in v1:
time: 1170 us; the launch traced here: 1160 us
  Pallas kernels  621 us (53%)
  waiting for transfers between devices  248 us (21%)
  blocking collectives  177 us (15%)
  local copies, waits for them, and re-layouts  43.8 us (4%)
  other arithmetic  42 us (4%)
  starting transfers between devices  17.1 us (1%)
  between operations  14.8 us (1%)
    pallas_call x8, Pallas kernels, run_experts(): pl.pallas_call(functools.partial(expert_kernel, first, capacity, rows_blk...  548 us
    all_to_all x1, blocking collectives, per_device(): dg = lax.all_to_all(dg, 'ep', 0, 0, tiled=True).reshape(experts, tok)  177 us
    ppermute x21, waiting for transfers between devices, swap(): return lax.ppermute(a, 'ep', [(i, i ^ mask) for i in range(ep_size)])  147 us
    pallas_call x4, Pallas kernels, run_combine(): pl.pallas_call(functools.partial(combine_kernel, len(dxs), tok - BACK, ca...  72.5 us
    reduce_scatter x2, waiting for transfers between devices, reduce_part(): lax.psum_scatter(acc[h][0], 'fsdp', scatter_dimension=0, tiled=False)  50.2 us
    all_gather x2, waiting for transfers between devices, per_device(): w_up.append(lax.all_gather(up_loc[h * half:(h + 1) * half], 'fsdp', axis=0))  28.3 us
  transfers between devices with their start and end apart: 30, of which 5 were waited for; matrix products, arithmetic and copies ran while one was open for 7% of the time, Pallas kernels for 47%

profile of v1, /device:TPU:0, one launch (start us, length us, event | category | flops | bytes accessed | tf_op | source)
XLA Modules:
  0.0 1163.8 jit_solution(15706368506649506167)
XLA Ops:
  7.2 1.0 bitcast_convert_fusion
  8.2 1.5 pad_maximum_fusion.1
  9.8 1.5 copy.43
  11.3 1.0 fusion.25
  12.7 1.5 fusion.24
  14.3 0.5 all-gather.15.cloned.1.call-update
  14.9 0.6 collective-permute-start
  15.4 2.6 collective-permute-start.3
  18.4 1.8 collective-permute-start.11
  20.4 20.3 %all-gather.11.cloned.1.call-done = f32[128,2048]{1,0:T(8,128)} async-done(((f32[16,2048]{1,0:T(8,128)}), f32[128,2048]{1,0:T(8,128)}) %all-gather.11.cloned.1.call-update) | async-done | bytes 1048592 | tf_op jit(solution)/shard_map/all_gather | solution.py:300
  40.7 1.8 gather_fusion
  42.8 0.8 compare_reduce_fusion
  44.0 0.7 fusion.7
  45.0 1.5 collective-permute-start.9
  46.5 67.2 %collective-permute-done.3.xa = bf16[2048,1024]{1,0:T(8,128)(2,1)} collective-permute-done((bf16[2048,1024]{1,0:T(8,128)(2,1)}, bf16[2048,1024]{1,0:T(8,128)(2,1)}, u32[]{:S(2)}, u32[]{:S(2)}) %collective-permute-start.3) | collective-permute-done | bytes 4194336 | tf_op jit(solution)/shard_map/ppermute | solution.py:267
  113.9 0.6 copy.87
  114.5 0.6 copy.85
  115.1 0.6 copy.83
  115.7 0.6 copy.81
  116.3 0.6 copy.88
  116.9 0.6 copy.86
  117.5 0.6 copy.84
  118.1 0.6 copy.82
  119.0 0.6 fusion.13
  119.7 0.6 slice_bitcast_fusion.22
  120.3 0.7 slice_bitcast_fusion.14
  121.0 2.1 collective-permute-start.15
  123.1 80.2 %collective-permute-done.5.ya = bf16[2048,1024]{1,0:T(8,128)(2,1)} collective-permute-done((bf16[2048,1024]{1,0:T(8,128)(2,1)}, bf16[2048,1024]{1,0:T(8,128)(2,1)}, u32[]{:S(2)}, u32[]{:S(2)}) %collective-permute-start.5) | collective-permute-done | bytes 4194336 | tf_op jit(solution)/shard_map/ppermute | solution.py:267
  203.3 1.7 collective-permute-start.17
  205.0 62.8 %experts.9 = (bf16[2,2,640,1024]{3,2,1,0:T(8,128)(2,1)}, f32[2,2,8,256]{3,2,1,0:T(8,128)}, f32[4,2,256,1024]{3,2,1,0:T(8,128)}, f32[4,2,256,512]{3,2,1,0:T(8,128)}) custom-call(s32[2,2,8]{2,1,0:T(2,128)} %get-tuple-element.130.starts, s32[2,2,8,256]{3,2,1,0:T(8,128)} %get-tuple-element.109.pos, f32[2,2,8,256]{3,2,1,0:T(8,128)} %bitcast.141, ...), custom_call_target="tpu_custom_call" | custom-call | flops 33285996544 | bytes 94371840 | tf_op jit(solution)/shard_map/experts/pallas_call | solution.py:169
  268.4 28.3 %all-gather.13.cloned.1.call-done = bf16[8,256,1024]{2,1,0:T(8,128)(2,1)} async-done(((bf16[2,256,1024]{2,1,0:T(8,128)(2,1)}), bf16[8,256,1024]{2,1,0:T(8,128)(2,1)}) %all-gather.13.cloned.1.call-update) | async-done | bytes 4194320 | tf_op jit(solution)/shard_map/all_gather | solution.py:295
  296.7 62.5 %experts.8 = (bf16[2,2,640,1024]{3,2,1,0:T(8,128)(2,1)}, f32[2,2,8,256]{3,2,1,0:T(8,128)}, f32[4,2,256,1024]{3,2,1,0:T(8,128)}, f32[4,2,256,512]{3,2,1,0:T(8,128)}) custom-call(s32[2,2,8]{2,1,0:T(2,128)} %get-tuple-element.137.starts, s32[2,2,8,256]{3,2,1,0:T(8,128)} %get-tuple-element.116.pos, f32[2,2,8,256]{3,2,1,0:T(8,128)} %bitcast.140, ...), custom_call_target="tpu_custom_call" | custom-call | flops 33285996544 | bytes 94371840 | tf_op jit(solution)/shard_map/experts/pallas_call | solution.py:169
  359.8 70.7 %experts.11 = (bf16[2,2,640,1024]{3,2,1,0:T(8,128)(2,1)}, f32[2,2,8,256]{3,2,1,0:T(8,128)}, f32[4,2,256,1024]{3,2,1,0:T(8,128)}, f32[4,2,256,512]{3,2,1,0:T(8,128)}) custom-call(s32[2,2,8]{2,1,0:T(2,128)} %get-tuple-element.135.starts, s32[2,2,8,256]{3,2,1,0:T(8,128)} %get-tuple-element.114.pos, f32[2,2,8,256]{3,2,1,0:T(8,128)} %bitcast.139, ...), custom_call_target="tpu_custom_call" | custom-call | flops 33285996544 | bytes 94371840 | tf_op jit(solution)/shard_map/experts/pallas_call | solution.py:169
  430.6 70.2 %experts.13 = (bf16[2,2,640,1024]{3,2,1,0:T(8,128)(2,1)}, f32[2,2,8,256]{3,2,1,0:T(8,128)}, f32[4,2,256,1024]{3,2,1,0:T(8,128)}, f32[4,2,256,512]{3,2,1,0:T(8,128)}) custom-call(s32[2,2,8]{2,1,0:T(2,128)} %get-tuple-element.133.starts, s32[2,2,8,256]{3,2,1,0:T(8,128)} %get-tuple-element.112.pos, f32[2,2,8,256]{3,2,1,0:T(8,128)} %bitcast.138, ...), custom_call_target="tpu_custom_call" | custom-call | flops 33285996544 | bytes 94371840 | tf_op jit(solution)/shard_map/experts/pallas_call | solution.py:169
  500.8 70.6 %experts.15 = (bf16[2,2,640,1024]{3,2,1,0:T(8,128)(2,1)}, f32[2,2,8,256]{3,2,1,0:T(8,128)}, f32[4,2,256,1024]{3,2,1,0:T(8,128)}, f32[4,2,256,512]{3,2,1,0:T(8,128)}) custom-call(s32[2,2,8]{2,1,0:T(2,128)} %get-tuple-element.131.starts, s32[2,2,8,256]{3,2,1,0:T(8,128)} %get-tuple-element.110.pos, f32[2,2,8,256]{3,2,1,0:T(8,128)} %bitcast.137, ...), custom_call_target="tpu_custom_call" | custom-call | flops 33285996544 | bytes 94371840 | tf_op jit(solution)/shard_map/experts/pallas_call | solution.py:169
  571.4 70.4 %experts.10 = (bf16[2,2,640,1024]{3,2,1,0:T(8,128)(2,1)}, f32[2,2,8,256]{3,2,1,0:T(8,128)}, f32[4,2,256,1024]{3,2,1,0:T(8,128)}, f32[4,2,256,512]{3,2,1,0:T(8,128)}) custom-call(s32[2,2,8]{2,1,0:T(2,128)} %get-tuple-element.136.starts, s32[2,2,8,256]{3,2,1,0:T(8,128)} %get-tuple-element.115.pos, f32[2,2,8,256]{3,2,1,0:T(8,128)} %bitcast.136, ...), custom_call_target="tpu_custom_call" | custom-call | flops 33285996544 | bytes 94371840 | tf_op jit(solution)/shard_map/experts/pallas_call | solution.py:169
  641.9 70.3 %experts.12 = (bf16[2,2,640,1024]{3,2,1,0:T(8,128)(2,1)}, f32[2,2,8,256]{3,2,1,0:T(8,128)}, f32[4,2,256,1024]{3,2,1,0:T(8,128)}, f32[4,2,256,512]{3,2,1,0:T(8,128)}) custom-call(s32[2,2,8]{2,1,0:T(2,128)} %get-tuple-element.134.starts, s32[2,2,8,256]{3,2,1,0:T(8,128)} %get-tuple-element.113.pos, f32[2,2,8,256]{3,2,1,0:T(8,128)} %bitcast.135, ...), custom_call_target="tpu_custom_call" | custom-call | flops 33285996544 | bytes 94371840 | tf_op jit(solution)/shard_map/experts/pallas_call | solution.py:169
  712.2 70.6 %experts.14 = (bf16[2,2,640,1024]{3,2,1,0:T(8,128)(2,1)}, f32[2,2,8,256]{3,2,1,0:T(8,128)}, f32[4,2,256,1024]{3,2,1,0:T(8,128)}, f32[4,2,256,512]{3,2,1,0:T(8,128)}) custom-call(s32[2,2,8]{2,1,0:T(2,128)} %get-tuple-element.132.starts, s32[2,2,8,256]{3,2,1,0:T(8,128)} %get-tuple-element.111.pos, f32[2,2,8,256]{3,2,1,0:T(8,128)} %bitcast.134, ...), custom_call_target="tpu_custom_call" | custom-call | flops 33285996544 | bytes 94371840 | tf_op jit(solution)/shard_map/experts/pallas_call | solution.py:169
  782.9 0.7 reduce-scatter.7.cloned.1.call-update
  783.6 0.7 reduce-scatter.5.cloned.1.call-update
  784.6 4.7 copy.41
  789.8 4.0 fusion.23
  793.8 18.1 %combine.5 = bf16[2,2048,1024]{2,1,0:T(8,128)(2,1)} custom-call(s32[2,4,9]{2,1,0:T(4,128)S(1)} %get-tuple-element.129.starts, s32[2,2048,4]{2,1,0:T(8,128)S(1)} %get-tuple-element.92.pos, bf16[2,2,640,1024]{3,2,1,0:T(8,128)(2,1)} %get-tuple-element.41.rest_0_, bf16[2,2,640,1024]{3,2,1,0:T(8,128)(2,1)} %get-tuple-element.44.rest_1_), custom_call_target="tpu_custom_call" | custom-call | flops 8589934592 | bytes 20971520 | tf_op jit(solution)/shard_map/combine/pallas_call | solution.py:226
  811.9 4.6 slice_bitcast_fusion.4
  816.6 18.0 %combine.6 = bf16[2,2048,1024]{2,1,0:T(8,128)(2,1)} custom-call(s32[2,4,9]{2,1,0:T(4,128)S(1)} %get-tuple-element.128.starts, s32[2,2048,4]{2,1,0:T(8,128)S(1)} %get-tuple-element.91.pos, bf16[2,2,640,1024]{3,2,1,0:T(8,128)(2,1)} %get-tuple-element.47.rest_0_, bf16[2,2,640,1024]{3,2,1,0:T(8,128)(2,1)} %get-tuple-element.50.rest_1_), custom_call_target="tpu_custom_call" | custom-call | flops 8589934592 | bytes 20971520 | tf_op jit(solution)/shard_map/combine/pallas_call | solution.py:226
  834.7 4.6 slice_bitcast_fusion.2
  839.7 18.0 %combine.7 = bf16[2,2048,1024]{2,1,0:T(8,128)(2,1)} custom-call(s32[2,4,9]{2,1,0:T(4,128)S(1)} %get-tuple-element.127.starts, s32[2,2048,4]{2,1,0:T(8,128)S(1)} %get-tuple-element.90.pos, bf16[2,2,640,1024]{3,2,1,0:T(8,128)(2,1)} %get-tuple-element.53.rest_0_, bf16[2,2,640,1024]{3,2,1,0:T(8,128)(2,1)} %get-tuple-element.56.rest_1_), custom_call_target="tpu_custom_call" | custom-call | flops 8589934592 | bytes 20971520 | tf_op jit(solution)/shard_map/combine/pallas_call | solution.py:226
  857.6 4.6 slice_bitcast_fusion
  862.3 18.4 %combine.4 = bf16[2,2048,1024]{2,1,0:T(8,128)(2,1)} custom-call(s32[2,4,9]{2,1,0:T(4,128)S(1)} %get-tuple-element.126.starts, s32[2,2048,4]{2,1,0:T(8,128)S(1)} %get-tuple-element.89.pos, bf16[2,2,640,1024]{3,2,1,0:T(8,128)(2,1)} %get-tuple-element.37.rest_0_, bf16[2,2,640,1024]{3,2,1,0:T(8,128)(2,1)} %get-tuple-element.38.rest_1_), custom_call_target="tpu_custom_call" | custom-call | flops 8589934592 | bytes 20971520 | tf_op jit(solution)/shard_map/combine/pallas_call | solution.py:226
  880.7 4.8 slice_bitcast_fusion.6
  886.0 7.8 fusion.2
  893.8 1.4 collective-permute-start.8
  895.2 6.3 fusion.1
  901.6 1.6 collective-permute-start.14
  903.2 4.2 fusion
  907.4 0.9 collective-permute-start.20
  908.6 0.8 gather_fusion.1
  909.6 177.1 %all_to_all.5 = f32[8,4,2048]{2,1,0:T(4,128)S(1)} all-to-all(f32[8,4,2048]{2,1,0:T(4,128)S(1)} %broadcast_select_fusion.1), channel_id=1, replica_groups=mesh['fsdp'=4,'ep'=8] {'ep'}, dimensions={0} | all-to-all | bytes 524288 | tf_op jit(solution)/shard_map/all_to_all | solution.py:366
  1086.8 1.0 select_reduce_fusion
  1087.8 1.7 maximum_bitcast_fusion
  1089.5 1.8 copy.45
  1091.3 11.0 fusion.6
  1102.3 50.2 %reduce-scatter.5.cloned.1.call-done = f32[1,2,256,1024]{3,2,1,0:T(8,128)} async-done(((f32[4,2,256,1024]{3,2,1,0:T(8,128)}), f32[1,2,256,1024]{3,2,1,0:T(8,128)}) %reduce-scatter.5.cloned.1.call-update) | async-done | bytes 2097168 | tf_op jit(solution)/shard_map/reduce_scatter | solution.py:350
  1152.5 4.6 pad_maximum_fusion
  (137 shorter events, 5.9 us)
Async XLA Ops:
  7.2 5.2 copy-start.2
  7.2 5.4 copy-start.3
  7.2 33.5 %all-gather.11.cloned.1.call-start = ((), (), s32[]{:S(2)}) async-start(), calls=%async_computation.9 | async-start | bytes 1179648 | tf_op jit(solution)/shard_map/all_gather | solution.py:300
  9.7 195.3 %all-gather.19.cloned.1.call-start = ((), (), s32[]{:S(2)}) async-start(), calls=%async_computation.13 | async-start | bytes 2621440 | tf_op jit(solution)/shard_map/all_gather | solution.py:296
  12.3 192.7 %all-gather.17.cloned.1.call-start = ((), (), s32[]{:S(2)}) async-start(), calls=%async_computation.12 | async-start | bytes 5242880 | tf_op jit(solution)/shard_map/all_gather | solution.py:295
  14.2 254.2 %all-gather.15.cloned.1.call-start = ((), (), s32[]{:S(2)}) async-start(), calls=%async_computation.11 | async-start | bytes 2621440 | tf_op jit(solution)/shard_map/all_gather | solution.py:296
  14.8 281.9 %all-gather.13.cloned.1.call-start = ((), (), s32[]{:S(2)}) async-start(), calls=%async_computation.10 | async-start | bytes 5242880 | tf_op jit(solution)/shard_map/all_gather | solution.py:295
  14.9 30.1 %collective-permute-start = (bf16[2048,1024]{1,0:T(8,128)(2,1)}, bf16[2048,1024]{1,0:T(8,128)(2,1)}, u32[]{:S(2)}, u32[]{:S(2)}) collective-permute-start(bf16[2048,1024]{1,0:T(8,128)(2,1)} %xa.3), channel_id=1, source_target_pairs={{0,1},{1,0},{2,3},{3,2},{4,5},{5,4},{6,7},{7,6},{8,9},{9,8},{10,11... | collective-permute-start | bytes 12582920 | tf_op jit(solution)/shard_map/ppermute | solution.py:267
  15.4 98.2 %collective-permute-start.3 = (bf16[2048,1024]{1,0:T(8,128)(2,1)}, bf16[2048,1024]{1,0:T(8,128)(2,1)}, u32[]{:S(2)}, u32[]{:S(2)}) collective-permute-start(bf16[2048,1024]{1,0:T(8,128)(2,1)} %xa.3), channel_id=1, source_target_pairs={{0,2},{1,3},{2,0},{3,1},{4,6},{5,7},{6,4},{7,5},{8,10},{9,11},{10,... | collective-permute-start | bytes 12582920 | tf_op jit(solution)/shard_map/ppermute | solution.py:267
  18.0 103.0 %collective-permute-start.1 = (bf16[2048,1024]{1,0:T(8,128)(2,1)}, bf16[2048,1024]{1,0:T(8,128)(2,1)}, u32[]{:S(2)}, u32[]{:S(2)}) collective-permute-start(bf16[2048,1024]{1,0:T(8,128)(2,1)} %ya.3), channel_id=1, source_target_pairs={{0,1},{1,0},{2,3},{3,2},{4,5},{5,4},{6,7},{7,6},{8,9},{9,8},{10,11... | collective-permute-start | bytes 12582920 | tf_op jit(solution)/shard_map/ppermute | solution.py:267
  18.2 185.1 %collective-permute-start.5 = (bf16[2048,1024]{1,0:T(8,128)(2,1)}, bf16[2048,1024]{1,0:T(8,128)(2,1)}, u32[]{:S(2)}, u32[]{:S(2)}) collective-permute-start(bf16[2048,1024]{1,0:T(8,128)(2,1)} %ya.3), channel_id=1, source_target_pairs={{0,2},{1,3},{2,0},{3,1},{4,6},{5,7},{6,4},{7,5},{8,10},{9,11},{10,... | collective-permute-start | bytes 12582920 | tf_op jit(solution)/shard_map/ppermute | solution.py:267
  18.4 184.8 %collective-permute-start.11 = (bf16[2048,1024]{1,0:T(8,128)(2,1)}, bf16[2048,1024]{1,0:T(8,128)(2,1)}, u32[]{:S(2)}, u32[]{:S(2)}) collective-permute-start(bf16[2048,1024]{1,0:T(8,128)(2,1)} %ya.3), channel_id=1, source_target_pairs={{0,4},{1,5},{2,6},{3,7},{4,0},{5,1},{6,2},{7,3},{8,12},{9,13},{10,... | collective-permute-start | bytes 12582920 | tf_op jit(solution)/shard_map/ppermute | solution.py:267
  20.2 1067.5 %reduce-scatter.11.cloned.1.call-start = ((), (), s32[]{:S(2)}) async-start(), calls=%async_computation.8 | async-start | bytes 5242880 | tf_op jit(solution)/shard_map/reduce_scatter | solution.py:351
  20.3 22.5 %copy-start.16 = (pred[8]{0:T(512)(128)(4,1)}, pred[8]{0:T(512)(128)(4,1)S(1)}, u32[]{:S(2)}) copy-start(pred[8]{0:T(512)(128)(4,1)S(1)} %compare_and_fusion) | copy-start | bytes 28
  20.4 22.4 %copy-start.15 = (s32[1024]{0:T(1024)}, s32[1024]{0:T(1024)S(1)}, u32[]{:S(2)}) copy-start(s32[1024]{0:T(1024)S(1)} %pad_clamp_fusion) | copy-start | bytes 12292
  45.0 222.9 %collective-permute-start.9 = (bf16[2048,1024]{1,0:T(8,128)(2,1)}, bf16[2048,1024]{1,0:T(8,128)(2,1)}, u32[]{:S(2)}, u32[]{:S(2)}) collective-permute-start(bf16[2048,1024]{1,0:T(8,128)(2,1)} %xa.3), channel_id=1, source_target_pairs={{0,4},{1,5},{2,6},{3,7},{4,0},{5,1},{6,2},{7,3},{8,12},{9,13},{10,... | collective-permute-start | bytes 12582920 | tf_op jit(solution)/shard_map/ppermute | solution.py:267
  113.6 154.5 %collective-permute-start.4 = (bf16[2048,1024]{1,0:T(8,128)(2,1)}, bf16[2048,1024]{1,0:T(8,128)(2,1)}, u32[]{:S(2)}, u32[]{:S(2)}) collective-permute-start(bf16[2048,1024]{1,0:T(8,128)(2,1)} %collective-permute-done.3.xa), channel_id=1, source_target_pairs={{0,1},{1,0},{2,3},{3,2},{4,5},{5,4},{6,7},{7,6},{8,9},{9,8},{10,11... | collective-permute-start | bytes 12582920 | tf_op jit(solution)/shard_map/ppermute | solution.py:267
  119.0 1.3 copy-start
  119.0 2.0 copy-start.4
  121.0 238.3 %collective-permute-start.15 = (bf16[2048,1024]{1,0:T(8,128)(2,1)}, bf16[2048,1024]{1,0:T(8,128)(2,1)}, u32[]{:S(2)}, u32[]{:S(2)}) collective-permute-start(bf16[2048,1024]{1,0:T(8,128)(2,1)} %collective-permute-done.3.xa), channel_id=1, source_target_pairs={{0,4},{1,5},{2,6},{3,7},{4,0},{5,1},{6,2},{7,3},{8,12},{9,13},{10,... | collective-permute-start | bytes 12582920 | tf_op jit(solution)/shard_map/ppermute | solution.py:267
  203.3 156.5 %collective-permute-start.6 = (bf16[2048,1024]{1,0:T(8,128)(2,1)}, bf16[2048,1024]{1,0:T(8,128)(2,1)}, u32[]{:S(2)}, u32[]{:S(2)}) collective-permute-start(bf16[2048,1024]{1,0:T(8,128)(2,1)} %collective-permute-done.5.ya), channel_id=1, source_target_pairs={{0,1},{1,0},{2,3},{3,2},{4,5},{5,4},{6,7},{7,6},{8,9},{9,8},{10,11... | collective-permute-start | bytes 12582920 | tf_op jit(solution)/shard_map/ppermute | solution.py:267
  203.3 156.0 %collective-permute-start.17 = (bf16[2048,1024]{1,0:T(8,128)(2,1)}, bf16[2048,1024]{1,0:T(8,128)(2,1)}, u32[]{:S(2)}, u32[]{:S(2)}) collective-permute-start(bf16[2048,1024]{1,0:T(8,128)(2,1)} %collective-permute-done.11.ya), channel_id=1, source_target_pairs={{0,2},{1,3},{2,0},{3,1},{4,6},{5,7},{6,4},{7,5},{8,10},{9,11},{10,... | collective-permute-start | bytes 12582920 | tf_op jit(solution)/shard_map/ppermute | solution.py:267
  267.8 162.7 %collective-permute-start.12 = (bf16[2048,1024]{1,0:T(8,128)(2,1)}, bf16[2048,1024]{1,0:T(8,128)(2,1)}, u32[]{:S(2)}, u32[]{:S(2)}) collective-permute-start(bf16[2048,1024]{1,0:T(8,128)(2,1)} %collective-permute-done.11.ya), channel_id=1, source_target_pairs={{0,1},{1,0},{2,3},{3,2},{4,5},{5,4},{6,7},{7,6},{8,9},{9,8},{10,11... | collective-permute-start | bytes 12582920 | tf_op jit(solution)/shard_map/ppermute | solution.py:267
  268.1 162.4 %collective-permute-start.10 = (bf16[2048,1024]{1,0:T(8,128)(2,1)}, bf16[2048,1024]{1,0:T(8,128)(2,1)}, u32[]{:S(2)}, u32[]{:S(2)}) collective-permute-start(bf16[2048,1024]{1,0:T(8,128)(2,1)} %collective-permute-done.9.xa), channel_id=1, source_target_pairs={{0,1},{1,0},{2,3},{3,2},{4,5},{5,4},{6,7},{7,6},{8,9},{9,8},{10,11... | collective-permute-start | bytes 12582920 | tf_op jit(solution)/shard_map/ppermute | solution.py:267
  359.2 141.5 %collective-permute-start.16 = (bf16[2048,1024]{1,0:T(8,128)(2,1)}, bf16[2048,1024]{1,0:T(8,128)(2,1)}, u32[]{:S(2)}, u32[]{:S(2)}) collective-permute-start(bf16[2048,1024]{1,0:T(8,128)(2,1)} %collective-permute-done.15.xa), channel_id=1, source_target_pairs={{0,1},{1,0},{2,3},{3,2},{4,5},{5,4},{6,7},{7,6},{8,9},{9,8},{10,11... | collective-permute-start | bytes 12582920 | tf_op jit(solution)/shard_map/ppermute | solution.py:267
  359.3 141.5 %collective-permute-start.18 = (bf16[2048,1024]{1,0:T(8,128)(2,1)}, bf16[2048,1024]{1,0:T(8,128)(2,1)}, u32[]{:S(2)}, u32[]{:S(2)}) collective-permute-start(bf16[2048,1024]{1,0:T(8,128)(2,1)} %collective-permute-done.17.ya), channel_id=1, source_target_pairs={{0,1},{1,0},{2,3},{3,2},{4,5},{5,4},{6,7},{7,6},{8,9},{9,8},{10,11... | collective-permute-start | bytes 12582920 | tf_op jit(solution)/shard_map/ppermute | solution.py:267
  571.4 516.4 %reduce-scatter.9.cloned.1.call-start = ((), (), s32[]{:S(2)}) async-start(), calls=%async_computation.7 | async-start | bytes 5242880 | tf_op jit(solution)/shard_map/reduce_scatter | solution.py:351
  782.8 319.5 %reduce-scatter.7.cloned.1.call-start = ((), (), s32[]{:S(2)}) async-start(), calls=%async_computation.6 | async-start | bytes 10485760 | tf_op jit(solution)/shard_map/reduce_scatter | solution.py:350
  783.6 368.9 %reduce-scatter.5.cloned.1.call-start = ((), (), s32[]{:S(2)}) async-start(), calls=%async_computation.5 | async-start | bytes 10485760 | tf_op jit(solution)/shard_map/reduce_scatter | solution.py:350
  783.6 1.0 copy-start.5
  783.6 1.0 copy-start.1
  816.6 69.4 %collective-permute-start.7 = (bf16[2048,1024]{1,0:T(8,128)(2,1)}, bf16[2048,1024]{1,0:T(8,128)(2,1)}, u32[]{:S(2)}, u32[]{:S(2)}) collective-permute-start(bf16[2048,1024]{1,0:T(8,128)(2,1)} %slice_bitcast_fusion.4), channel_id=1, source_target_pairs={{0,1},{1,0},{2,3},{3,2},{4,5},{5,4},{6,7},{7,6},{8,9},{9,8},{10,11... | collective-permute-start | bytes 12582920 | tf_op jit(solution)/shard_map/ppermute | solution.py:267
  839.2 56.0 %collective-permute-start.13 = (bf16[2048,1024]{1,0:T(8,128)(2,1)}, bf16[2048,1024]{1,0:T(8,128)(2,1)}, u32[]{:S(2)}, u32[]{:S(2)}) collective-permute-start(bf16[2048,1024]{1,0:T(8,128)(2,1)} %slice_bitcast_fusion.2), channel_id=1, source_target_pairs={{0,1},{1,0},{2,3},{3,2},{4,5},{5,4},{6,7},{7,6},{8,9},{9,8},{10,11... | collective-permute-start | bytes 12582920 | tf_op jit(solution)/shard_map/ppermute | solution.py:267
  862.3 40.9 %collective-permute-start.19 = (bf16[2048,1024]{1,0:T(8,128)(2,1)}, bf16[2048,1024]{1,0:T(8,128)(2,1)S(1)}, u32[]{:S(2)}, u32[]{:S(2)}) collective-permute-start(bf16[2048,1024]{1,0:T(8,128)(2,1)} %slice_bitcast_fusion), channel_id=1, source_target_pairs={{0,1},{1,0},{2,3},{3,2},{4,5},{5,4},{6,7},{7,6},{8,9},{9,8},{10,11... | collective-permute-start | bytes 12582920 | tf_op jit(solution)/shard_map/ppermute | solution.py:267
  880.7 14.5 %slice-start.2 = ((s8[8388608]{0:T(1024)(128)(4,1)}), s8[4194304]{0:T(1024)(128)(4,1)S(1)}, s32[]{:S(2)}) async-start(s8[8388608]{0:T(1024)(128)(4,1)} %bitcast.123), calls=%async_computation.16 | async-start | bytes 8388608
  885.5 9.7 slice-start.3
  885.5 205.8 %collective-permute-start.2 = (bf16[2048,1024]{1,0:T(8,128)(2,1)}, bf16[2048,1024]{1,0:T(8,128)(2,1)}, u32[]{:S(2)}, u32[]{:S(2)}) collective-permute-start(bf16[2048,1024]{1,0:T(8,128)(2,1)} %slice_bitcast_fusion.6), channel_id=1, source_target_pairs={{0,1},{1,0},{2,3},{3,2},{4,5},{5,4},{6,7},{7,6},{8,9},{9,8},{10,11... | collective-permute-start | bytes 12582920 | tf_op jit(solution)/shard_map/ppermute | solution.py:267
  886.0 17.2 %slice-start = ((s8[8388608]{0:T(1024)(128)(4,1)}), s8[4194304]{0:T(1024)(128)(4,1)S(1)}, s32[]{:S(2)}) async-start(s8[8388608]{0:T(1024)(128)(4,1)} %bitcast.121), calls=%async_computation.14 | async-start | bytes 8388608
  893.8 9.3 slice-start.1
  893.8 197.5 %collective-permute-start.8 = (bf16[2048,1024]{1,0:T(8,128)(2,1)}, bf16[2048,1024]{1,0:T(8,128)(2,1)}, u32[]{:S(2)}, u32[]{:S(2)}) collective-permute-start(bf16[2048,1024]{1,0:T(8,128)(2,1)} %fusion.2), channel_id=1, source_target_pairs={{0,2},{1,3},{2,0},{3,1},{4,6},{5,7},{6,4},{7,5},{8,10},{9,11},{10,... | collective-permute-start | bytes 12582920 | tf_op jit(solution)/shard_map/ppermute | solution.py:267
  901.5 6.8 copy-start.7
  901.5 6.8 copy-start.8
  901.5 6.8 copy-start.9
  901.5 6.8 copy-start.10
  901.5 6.8 copy-start.11
  901.5 6.8 copy-start.12
  901.5 6.8 copy-start.13
  901.5 6.8 copy-start.14
  901.5 7.9 copy-start.17
  901.6 185.2 %copy-start.6 = (s32[2048,8]{0,1:T(8,128)S(1)}, s32[2048,8]{0,1:T(8,128)}, u32[]{:S(2)}) copy-start(s32[2048,8]{0,1:T(8,128)} %param.9) | copy-start | bytes 196612
  901.6 189.8 %collective-permute-start.14 = (bf16[2048,1024]{1,0:T(8,128)(2,1)}, bf16[2048,1024]{1,0:T(8,128)(2,1)}, u32[]{:S(2)}, u32[]{:S(2)}) collective-permute-start(bf16[2048,1024]{1,0:T(8,128)(2,1)} %fusion.1), channel_id=1, source_target_pairs={{0,4},{1,5},{2,6},{3,7},{4,0},{5,1},{6,2},{7,3},{8,12},{9,13},{10,... | collective-permute-start | bytes 12582920 | tf_op jit(solution)/shard_map/ppermute | solution.py:267
  907.4 183.9 %collective-permute-start.20 = (bf16[2048,1024]{1,0:T(8,128)(2,1)}, bf16[2048,1024]{1,0:T(8,128)(2,1)}, u32[]{:S(2)}, u32[]{:S(2)}) collective-permute-start(bf16[2048,1024]{1,0:T(8,128)(2,1)} %fusion), channel_id=1, source_target_pairs={{0,6},{1,7},{2,4},{3,5},{4,2},{5,3},{6,0},{7,1},{8,14},{9,15},{10,... | collective-permute-start | bytes 12582920 | tf_op jit(solution)/shard_map/ppermute | solution.py:267
Sparse Core Ops, SparseCore 0:
  9.9 30.7 all-gather.10
  42.8 45.2 all-gather.18
  90.3 79.1 all-gather.16
  171.5 43.9 all-gather.14
  217.5 79.1 all-gather.12
  571.5 75.3 reduce-scatter.10
  782.9 75.3 reduce-scatter.8
  860.7 144.7 reduce-scatter.6
  1007.8 144.6 reduce-scatter.4
